TPU v7x, 128 devices: a whole 4x4x4 slice. The times are simulated.
128 devices in a mesh: slab: 32 (over z, x, core), pen: 4 (over y).
Axes of the slice: x: 4, y: 4, z: 4, core: 2. Of those that a mesh axis runs over, the one named last changes fastest.
Arguments:
- pressure: float32 [512, 512, 512], P('slab', 'pen'), may hold values from -6 to 6
- previous: float32 [512, 512, 512], P('slab', 'pen'), may hold values from -6 to 6
- speed_ratio: float32 [512, 512, 512], P('slab', 'pen'), may hold values from 0.25 to 1
- traces: float32 [2, 2048], P(None, ('slab', 'pen')), may hold values from -6 to 6
- sensor_voxels: int32 [3, 2048], replicated, may hold values from 0 to 511, as said below
- trace_column: int32 [2048], replicated, may hold values from 0 to 2047, each once
Outputs:
- final_pressure: float32 [512, 512, 512], P('slab', 'pen')
- prior_pressure: float32 [512, 512, 512], P('slab', 'pen')
Inputs may be any that keep to these rules, and one draw needn't show every extreme that they name: `sensor_voxels`: row 0 holds each sensor's z cell (below 512), row 1 its y cell (below 512), row 2 its x cell (below 512); no two sensors share a y, x pair. `trace_column`: each of the 2048 trace columns belongs to exactly one sensor.
All inputs are finite; a program needn't handle non-finite values.
Results may differ from a plain program's by a relative error of at most 0.0001.
Values sent between devices are 32-bit elements; how exact they have to be, the bound alone decides.
No kernel may reach another device: no remote copies, remote signals or barrier semaphores. Data moves between devices by JAX's collectives and lax.ppermute only.
A program may use at most 128 MiB of HBM per device.

v0:
```python
import math

import jax
import jax.numpy as jnp
import numpy as np
from jax import lax
from jax.experimental import pallas as pl
from jax.experimental.pallas import tpu as pltpu
from jax.sharding import Mesh
from jax.sharding import PartitionSpec as P

NX = 512
NY = 512
NZ = 512
HALF = 256
SENSORS = 2048
SLAB = ("slab_0", "slab_1", "slab_2")
SLAB_PEN = ("slab_0", "slab_1", "slab_2", "pen")
HALF_CFL = 0.25
MIB = 1024 * 1024
ZB = 16
PZ = 2
F32 = jnp.float32
BF16 = jnp.bfloat16


def half_tables():
    m = np.arange(HALF)[:, None]
    n = np.arange(HALF)[None, :]
    parts = []
    for freq in (2 * m, 2 * m + 1):
        angle = (freq * n % 512) * (2.0 * math.pi / 512)
        parts.append(np.cos(angle) + np.sin(angle))
    even, odd = parts
    stack = []
    for table in (even, odd, odd.T):
        high = table.astype(BF16)
        low = (table - high.astype(np.float64)).astype(BF16)
        stack += [high, low]
    return np.stack(stack)


EVEN, ODD, ODD_T = 0, 2, 4


def split(x):
    high = x.astype(BF16)
    low = (x - high.astype(F32)).astype(BF16)
    return high, low


def split3(x, axis):
    high, low = split(x)
    return jnp.concatenate([high, low, high], axis=axis)


def table3(tab, which, axis):
    high = tab[which]
    return jnp.concatenate([high, high, tab[which + 1]], axis=axis)


def dot(left, right, dims):
    return lax.dot_general(left, right, (dims, ((), ())), preferred_element_type=F32)


def fill_maps(offs, vox, tcol, gathered, zmap, vmap0, vmap1):
    z = vox[0:1, :] - offs[0]
    y = vox[1:2, :] - offs[1]
    tile = tcol[...] // 16
    lane = tcol[...] % 16
    inside = (z >= 0) & (z < 16) & (y >= 0) & (y < 128)
    y = jnp.where(inside, y, -1)
    rows128 = lax.broadcasted_iota(jnp.int32, (128, SENSORS), 0)
    pick = (rows128 == tile).astype(F32).astype(BF16)
    g = gathered[...].T
    g0, g1 = split(g)
    g2 = (g - g0.astype(F32) - g1.astype(F32)).astype(BF16)
    parts = dot(jnp.concatenate([g0, g1, g2], axis=0), pick, ((1,), (0,)))
    spread = parts[0:32] + parts[32:64] + parts[64:96]
    rows16 = lax.broadcasted_iota(jnp.int32, (16, SENSORS), 0)
    here = rows16 == lane
    onrow = rows128 == y
    lhs = [jnp.where(onrow, (z + 1).astype(F32), 0.0).astype(BF16)]
    for t in range(2):
        value = jnp.sum(jnp.where(here, spread[16 * t : 16 * t + 16], 0.0), axis=0, keepdims=True)
        v0 = value.astype(BF16).astype(F32)
        v1 = (value - v0).astype(BF16).astype(F32)
        v2 = value - v0 - v1
        for part in (v0, v1, v2):
            lhs.append(jnp.where(onrow, part, 0.0).astype(BF16))
    columns = lax.broadcasted_iota(jnp.int32, (NX, SENSORS), 0)
    oncol = (columns == vox[2:3, :]).astype(F32).astype(BF16)
    out = dot(jnp.concatenate(lhs, axis=0), oncol, ((1,), (1,)))
    zmap[...] = out[0:128].astype(jnp.int32) - 1
    vmap0[...] = out[128:256] + out[256:384] + out[384:512]
    vmap1[...] = out[512:640] + out[640:768] + out[768:896]


def to_y(a, b, tab):
    return [
        dot(split3(data, 1), table3(tab, which, 0), ((1,), (0,)))
        for which, data in ((EVEN, a + b), (ODD_T, a - b))
    ]


def to_z(by_y, tab):
    by_z = []
    for x in by_y:
        top, bottom = x[:HALF], x[HALF:]
        by_z.append(dot(table3(tab, EVEN, 1), split3(top + bottom, 0), ((1,), (0,))))
        by_z.append(dot(table3(tab, ODD, 1), split3(top - bottom, 0), ((1,), (0,))))
    return by_z


def quarter(i):
    return pl.ds(i % 2 * HALF, HALF), pl.ds(i // 2 * HALF, HALF)


def forward_x(cur, tab, out):
    sums = []
    for piece in cur:
        flat = piece.reshape(PZ * 128, NX)
        sums.append((flat[:, :HALF] + flat[:, HALF:], flat[:, :HALF] - flat[:, HALF:]))
    got = [
        [dot(table3(tab, (EVEN, ODD)[part], 1), split3(pair[part], 1), ((1,), (1,))) for part in range(2)]
        for pair in sums
    ]
    for i, pair in enumerate(got):
        for part in range(2):
            pieces = [pair[part][:, z * 128 : (z + 1) * 128].reshape(64, 4, 128) for z in range(2)]
            out[pl.ds(part * 64, 64), pl.ds(i * 8, 8), :] = jnp.concatenate(pieces, axis=1)


def inverse_x(arr, tab):
    halves = []
    for i in range(ZB // PZ):
        parts = []
        for part, which in enumerate((EVEN, ODD)):
            block = arr[pl.ds(part * 64, 64), pl.ds(i * 8, 8), :]
            pieces = [block[:, z * 4 : z * 4 + 4].reshape(HALF, 128) for z in range(2)]
            data = jnp.concatenate(pieces, axis=1)
            parts.append(dot(split3(data.T, 1), table3(tab, which, 0), ((1,), (0,))))
        halves.append(parts)
    return [
        jnp.concatenate([even + odd, even - odd], axis=1).reshape(PZ, 128, NX) for even, odd in halves
    ]


def planes(i):
    return pl.ds(i * PZ, PZ)


def here(zmap, i):
    z = lax.broadcasted_iota(jnp.int32, (PZ, 1, 1), 0) + ZB * pl.program_id(0) + i * PZ
    return zmap[...][None] == z


def first_kernel(offs, vox, tcol, gathered, p, tab, zmap, vmap0, vmap1, out, p_v, sems):
    step = pl.program_id(0)

    def copy(i):
        part = pl.ds(i * ZB, ZB)
        return pltpu.make_async_copy(p.at[part], p_v.at[part], sems.at[i])

    @pl.when(step == 0)
    def _():
        for i in range(16 // ZB):
            copy(i).start()
        fill_maps(offs, vox, tcol, gathered, zmap, vmap0, vmap1)

    copy(step).wait()
    base = step * ZB
    forward_x(
        [
            jnp.where(here(zmap, i), vmap0[...][None], p_v[pl.ds(base + i * PZ, PZ)])
            for i in range(ZB // PZ)
        ],
        tab,
        out,
    )


def write_back(scratch, target, sems, i):
    group = pl.program_id(0) * (ZB // PZ) + i
    part = pl.ds(group * PZ, PZ)
    return pltpu.make_async_copy(scratch.at[part], target.at[part], sems.at[group])


def wait_all(scratch, target, sems):
    @pl.when(pl.program_id(0) == 16 // ZB - 1)
    def _():
        for group in range(16 // PZ):
            part = pl.ds(group * PZ, PZ)
            pltpu.make_async_copy(scratch.at[part], target.at[part], sems.at[group]).wait()


def own_planes(i):
    return pl.ds(pl.program_id(0) * ZB + i * PZ, PZ)


def middle_kernel(arr, prev, speed, p, zmap, vmap0, vmap1, tab, cur_out, out, cur_v, sems):
    current = []
    for i, update in enumerate(inverse_x(arr, tab)):
        hit = here(zmap, i)
        now = jnp.where(hit, vmap0[...][None], p[planes(i)])
        following = 2.0 * now - prev[planes(i)] + speed[planes(i)] * update
        cur = jnp.where(hit, vmap1[...][None], following)
        cur_v[own_planes(i)] = cur
        write_back(cur_v, cur_out, sems, i).start()
        current.append(cur)
    forward_x(current, tab, out)
    wait_all(cur_v, cur_out, sems)


def last_kernel(arr, cur, speed, p, zmap, vmap0, tab, final, final_v, sems):
    for i, update in enumerate(inverse_x(arr, tab)):
        before = jnp.where(here(zmap, i), vmap0[...][None], p[planes(i)])
        final_v[own_planes(i)] = 2.0 * cur[planes(i)] - before + speed[planes(i)] * update
        write_back(final_v, final, sems, i).start()
    wait_all(final_v, final, sems)


def spectral_kernel(arr, sym, tab, out):
    step = pl.program_id(0)
    by_z = analyse(arr, tab, step)
    for j in range(2):
        for i in range(4):
            rows_of, cols_of = quarter(i)
            by_z[4 * j + i] = by_z[4 * j + i] * sym[j, rows_of, cols_of]
    synthesise(by_z, tab, out, step)


def analyse(arr, tab, step):
    by_y = []
    for j in range(2):
        k = step * 2 + j
        pens = [arr[:, p, pl.ds(k, 16, stride=4), :].reshape(512, 128) for p in range(4)]
        by_y += to_y(jnp.concatenate(pens[:2], axis=1), jnp.concatenate(pens[2:], axis=1), tab)
    return to_z(by_y, tab)


def synthesise(scaled, tab, out, step):
    back_z = [
        dot(table3(tab, (EVEN, ODD_T)[i % 2], 1), split3(x, 0), ((1,), (0,)))
        for i, x in enumerate(scaled)
    ]
    back_y = []
    for part in range(4):
        even, odd = back_z[2 * part], back_z[2 * part + 1]
        z = jnp.concatenate([even + odd, even - odd], axis=0)
        back_y.append(dot(split3(z, 1), table3(tab, (EVEN, ODD)[part % 2], 0), ((1,), (0,))))
    for j in range(2):
        a = back_y[2 * j] + back_y[2 * j + 1]
        b = back_y[2 * j] - back_y[2 * j + 1]
        for p in range(4):
            piece = (a, b)[p // 2][:, (p % 2) * 128 : (p % 2) * 128 + 128]
            out[:, p, pl.ds(step * 2 + j, 16, stride=4), :] = piece.reshape(32, 16, 128)


def whole(*shape):
    return pl.BlockSpec(shape, lambda i: (0,) * len(shape))


def pairs():
    return pl.BlockSpec((ZB, 128, NX), lambda i: (i, 0, 0))


def packed():
    return pl.BlockSpec((128, 4 * ZB, 128), lambda i: (0, i, 0))


def params(mib):
    return pltpu.CompilerParams(vmem_limit_bytes=mib * MIB)


TAB = whole(6, HALF, HALF)
MAP = whole(128, NX)
WIRE = jax.ShapeDtypeStruct((128, 64, 128), F32)


def squared_freq(indices, length):
    signed_index = jnp.where(2 * indices > length, indices - length, indices)
    angular = signed_index.astype(F32) * (2.0 * math.pi / length)
    return angular * angular


def half_order(rows):
    return jnp.where(rows < HALF, 2 * rows, 2 * (rows - HALF) + 1)


def local_freq(device):
    return half_order(device * 4 + jnp.arange(4, dtype=jnp.int32))


def symbol_of(device):
    rows = jnp.arange(512, dtype=jnp.int32)
    freq = squared_freq(half_order(rows), 512)
    freq_x = squared_freq(local_freq(device), NX)
    total = freq[None, :, None] + freq[None, None, :] + freq_x[:, None, None]
    square = total * (HALF_CFL * HALF_CFL)
    ratio = jnp.full_like(square, 1.0 / math.factorial(15) * -1.0)
    for n in (13, 11, 9, 7, 5, 3, 1):
        sign = 1.0 if n % 4 == 1 else -1.0
        ratio = ratio * square + sign / math.factorial(n)
    scale = -4.0 / (NX * NY * NZ)
    return square * ratio * ratio * scale


def in_hbm(array):
    return pltpu.with_memory_space_constraint(array, pltpu.HBM)


def exchange(array):
    return lax.all_to_all(array, SLAB_PEN, split_axis=0, concat_axis=0, tiled=True)


def step_pair(pressure, previous, speed_ratio, traces, sensor_voxels, trace_column):
    slab_index = lax.axis_index(SLAB)
    pen_index = lax.axis_index("pen")
    device = slab_index * 4 + pen_index
    tab = jnp.asarray(half_tables())
    offs = jnp.stack([slab_index * 16, pen_index * 128]).astype(jnp.int32)
    gathered = exchange(jnp.broadcast_to(traces[None], (128, 2, 16)))
    sym = symbol_of(device)
    in_smem = pl.BlockSpec(memory_space=pltpu.SMEM)
    map_type = jax.ShapeDtypeStruct((128, NX), F32)
    zmap, vmap0, vmap1, wire = pl.pallas_call(
        first_kernel,
        grid=(16 // ZB,),
        in_specs=[in_smem, whole(3, SENSORS), whole(1, SENSORS), whole(128, 32), pl.BlockSpec(memory_space=pl.ANY), TAB],
        out_specs=(MAP, MAP, MAP, packed()),
        out_shape=(jax.ShapeDtypeStruct((128, NX), jnp.int32), map_type, map_type, WIRE),
        scratch_shapes=[pltpu.VMEM((16, 128, NX), F32), pltpu.SemaphoreType.DMA((16 // ZB,))],
        compiler_params=params(24),
        name="first",
    )(
        offs,
        sensor_voxels,
        trace_column.reshape(1, SENSORS),
        gathered.reshape(128, 32),
        in_hbm(pressure),
        tab,
    )
    cube = whole(32, 4, 64, 128)
    planes2 = pl.BlockSpec((2, 512, 512), lambda i: (i, 0, 0))

    def spectral(arr):
        return pl.pallas_call(
            spectral_kernel,
            grid=(2,),
            in_specs=[cube, planes2, TAB],
            out_specs=cube,
            out_shape=jax.ShapeDtypeStruct((32, 4, 64, 128), F32),
            compiler_params=params(24),
            name="spectral",
        )(arr.reshape(32, 4, 64, 128), sym, tab).reshape(128, 64, 128)

    arr = exchange(spectral(exchange(wire)))
    current, wire = pl.pallas_call(
        middle_kernel,
        grid=(16 // ZB,),
        in_specs=[packed(), pairs(), pairs(), pairs(), MAP, MAP, MAP, TAB],
        out_specs=(pl.BlockSpec(memory_space=pl.ANY), packed()),
        out_shape=(pltpu.HBM((16, 128, NX), F32), WIRE),
        scratch_shapes=[pltpu.VMEM((16, 128, NX), F32), pltpu.SemaphoreType.DMA((16 // PZ,))],
        compiler_params=params(24),
        name="middle",
    )(arr, previous, speed_ratio, pressure, zmap, vmap0, vmap1, tab)
    arr = exchange(spectral(exchange(wire)))
    final = pl.pallas_call(
        last_kernel,
        grid=(16 // ZB,),
        in_specs=[packed(), pairs(), pairs(), pairs(), MAP, MAP, TAB],
        out_specs=pl.BlockSpec(memory_space=pl.ANY),
        out_shape=pltpu.HBM((16, 128, NX), F32),
        scratch_shapes=[pltpu.VMEM((16, 128, NX), F32), pltpu.SemaphoreType.DMA((16 // PZ,))],
        compiler_params=params(24),
        name="last",
    )(arr, current, speed_ratio, pressure, zmap, vmap0, tab)
    return (final, current)


def solution(mesh):
    torus = Mesh(
        mesh.devices.reshape(4, 4, 2, mesh.shape["pen"]), ("slab_0", "slab_1", "slab_2", "pen")
    )
    placed = (
        P(SLAB, "pen", None),
        P(SLAB, "pen", None),
        P(SLAB, "pen", None),
        P(None, SLAB_PEN),
        P(),
        P(),
    )
    return jax.shard_map(
        step_pair,
        mesh=torus,
        in_specs=placed,
        out_specs=(P(SLAB, "pen", None), P(SLAB, "pen", None)),
        check_vma=False,
    )
```

profile of v0, /device:TPU:1, one launch (start us, length us, event | category | flops | bytes accessed | tf_op | source)
XLA Modules:
  0.0 290.8 jit_solution(7600724428848716920)
XLA Ops:
  0.6 1.4 broadcast_in_dim.2
  2.0 11.5 %all-to-all-start = ((f32[128,2,16]{2,1,0:T(2,128)}), f32[128,2,16]{2,1,0:T(2,128)S(1)}, u32[]{:S(2)}, u32[]{:S(2)}) async-start(f32[128,2,16]{2,1,0:T(2,128)} %broadcast_in_dim.2), calls=%async_computation | async-start | bytes 262144 | tf_op jit(solution)/shard_map/all_to_all | solution.py:314
  13.5 0.1 pad_add_fusion.offs
  13.6 9.7 %all-to-all-done = f32[128,2,16]{2,1,0:T(2,128)S(1)} async-done(((f32[128,2,16]{2,1,0:T(2,128)}), f32[128,2,16]{2,1,0:T(2,128)S(1)}, u32[]{:S(2)}, u32[]{:S(2)}) %all-to-all-start) | async-done | bytes 16416 | tf_op jit(solution)/shard_map/all_to_all | solution.py:314
  23.3 0.1 copy.10
  23.4 0.1 copy.11.gathered
  23.5 0.0 copy-start.3
  23.5 1.1 copy-done.3
  24.6 0.0 copy-start.9
  24.6 0.8 copy-done.9
  25.4 0.0 copy-start.10
  25.4 0.7 copy-done.10
  26.1 5.0 %first.1 = (s32[128,512]{1,0:T(8,128)S(1)}, f32[128,512]{1,0:T(8,128)S(1)}, f32[128,512]{1,0:T(8,128)S(1)}, f32[128,64,128]{2,1,0:T(8,128)S(1)}) custom-call(s32[2]{0:T(128)S(1)} %pad_add_fusion.offs, s32[3,2048]{1,0:T(4,128)S(1)} %copy-done.9, s32[1,2048]{1,0:T(1,128)S(1)} %bitcast.11, f32[128,32]{1,0:T(8,128)S(1)} %copy.11.gathered, f32[16,128,512]{2,1,0:T(8,128)} %p.5, ...), custom_call_target="tpu_custom_call" | custom-call | tf_op jit(solution)/shard_map/first/pallas_call | solution.py:327
  31.1 0.0 copy-start.6
  31.1 2.0 copy-done.6
  33.1 5.2 %all-to-all-start.1 = ((f32[128,64,128]{2,1,0:T(8,128)}), f32[128,64,128]{2,1,0:T(8,128)}, u32[]{:S(2)}, u32[]{:S(2)}) async-start(f32[128,64,128]{2,1,0:T(8,128)} %copy-done.6), calls=%async_computation.1 | async-start | bytes 8388608 | tf_op jit(solution)/shard_map/all_to_all | solution.py:314
  38.4 0.0 copy-start.4
  38.5 0.1 broadcast_add_fusion
  38.6 4.1 %fusion.13.sym = f32[4,512,512]{2,1,0:T(8,128)} fusion(f32[4]{0:T(128)S(1)} %multiply_multiply_fusion.1, f32[512,512]{1,0:T(8,128)S(1)} %broadcast_add_fusion), kind=kLoop, calls=%fused_computation.16 | loop fusion | flops 19922944 | bytes 5242896 | tf_op jit(solution)/shard_map/mul | solution.py:306
  42.7 48.7 %all-to-all-done.1 = f32[128,64,128]{2,1,0:T(8,128)} async-done(((f32[128,64,128]{2,1,0:T(8,128)}), f32[128,64,128]{2,1,0:T(8,128)}, u32[]{:S(2)}, u32[]{:S(2)}) %all-to-all-start.1) | async-done | bytes 4194336 | tf_op jit(solution)/shard_map/all_to_all | solution.py:314
  91.4 0.0 copy-done.4
  91.4 0.0 copy-start
  91.4 2.2 copy-done
  93.6 0.0 copy-start.7
  93.6 9.9 %spectral.2 = f32[32,4,64,128]{3,2,1,0:T(8,128)S(1)} custom-call(f32[32,4,64,128]{3,2,1,0:T(8,128)} %bitcast.4.arr, f32[4,512,512]{2,1,0:T(8,128)S(1)} %copy-done, bf16[6,256,256]{2,1,0:T(8,128)(2,1)S(1)} %copy-done.4), custom_call_target="tpu_custom_call" | custom-call | tf_op jit(solution)/shard_map/spectral/pallas_call | solution.py:348
  103.5 0.0 copy-start.2
  103.5 0.0 copy-start.5
  103.5 56.9 %all_to_all.25.arr = f32[128,64,128]{2,1,0:T(8,128)S(1)} all-to-all(f32[128,64,128]{2,1,0:T(8,128)S(1)} %bitcast.10), channel_id=1, replica_groups=mesh['slab_0'=4,'slab_1'=4,'slab_2'=2,'pen'=4] {'slab_0','slab_1','slab_..., dimensions={0} | all-to-all | bytes 8388608 | tf_op jit(solution)/shard_map/all_to_all | solution.py:314
  160.4 0.0 copy-done.7
  160.4 0.0 copy-done.2
  160.4 0.0 copy-done.5
  160.4 5.1 %middle.1 = (f32[16,128,512]{2,1,0:T(8,128)}, f32[128,64,128]{2,1,0:T(8,128)S(1)}) custom-call(f32[128,64,128]{2,1,0:T(8,128)S(1)} %all_to_all.25.arr, f32[16,128,512]{2,1,0:T(8,128)S(1)} %copy-done.7, f32[16,128,512]{2,1,0:T(8,128)S(1)} %copy-done.5, f32[16,128,512]{2,1,0:T(8,128)S(1)} %copy-done.2, s32[128,512]{1,0:T(8,128)S(1)} %get-tuple-element.9.zmap, ...), custom_call_target="tpu_custom_call" | custom-call | tf_op jit(solution)/shard_map/middle/pallas_call | solution.py:359
  165.6 0.0 copy-start.1
  165.6 56.9 %all_to_all.26 = f32[128,64,128]{2,1,0:T(8,128)S(1)} all-to-all(f32[128,64,128]{2,1,0:T(8,128)S(1)} %get-tuple-element.12), channel_id=1, replica_groups=mesh['slab_0'=4,'slab_1'=4,'slab_2'=2,'pen'=4] {'slab_0','slab_1','slab_..., dimensions={0} | all-to-all | bytes 8388608 | tf_op jit(solution)/shard_map/all_to_all | solution.py:314
  222.5 0.0 copy-done.1
  222.5 7.5 %spectral.3 = f32[32,4,64,128]{3,2,1,0:T(8,128)S(1)} custom-call(f32[32,4,64,128]{3,2,1,0:T(8,128)S(1)} %bitcast.8, f32[4,512,512]{2,1,0:T(8,128)S(1)} %copy-done.1, bf16[6,256,256]{2,1,0:T(8,128)(2,1)S(1)} %copy-done.4), custom_call_target="tpu_custom_call" | custom-call | tf_op jit(solution)/shard_map/spectral/pallas_call | solution.py:348
  230.0 0.0 copy-start.8
  230.0 56.9 %all_to_all.27.arr = f32[128,64,128]{2,1,0:T(8,128)S(1)} all-to-all(f32[128,64,128]{2,1,0:T(8,128)S(1)} %bitcast.9), channel_id=1, replica_groups=mesh['slab_0'=4,'slab_1'=4,'slab_2'=2,'pen'=4] {'slab_0','slab_1','slab_..., dimensions={0} | all-to-all | bytes 8388608 | tf_op jit(solution)/shard_map/all_to_all | solution.py:314
  287.0 0.0 copy-done.8
  287.0 3.7 %last.1 = f32[16,128,512]{2,1,0:T(8,128)} custom-call(f32[128,64,128]{2,1,0:T(8,128)S(1)} %all_to_all.27.arr, f32[16,128,512]{2,1,0:T(8,128)S(1)} %copy-done.8, f32[16,128,512]{2,1,0:T(8,128)S(1)} %copy-done.5, f32[16,128,512]{2,1,0:T(8,128)S(1)} %copy-done.2, s32[128,512]{1,0:T(8,128)S(1)} %get-tuple-element.9.zmap, ...), custom_call_target="tpu_custom_call" | custom-call | tf_op jit(solution)/shard_map/last/pallas_call | solution.py:370
  (2 shorter events, 0.0 us)
Async XLA Ops:
  2.0 21.3 %all-to-all-start = ((f32[128,2,16]{2,1,0:T(2,128)}), f32[128,2,16]{2,1,0:T(2,128)S(1)}, u32[]{:S(2)}, u32[]{:S(2)}) async-start(f32[128,2,16]{2,1,0:T(2,128)} %broadcast_in_dim.2), calls=%async_computation | async-start | bytes 262144 | tf_op jit(solution)/shard_map/all_to_all | solution.py:314
  23.5 1.1 copy-start.3
  24.6 0.8 copy-start.9
  25.4 0.7 copy-start.10
  31.1 2.0 copy-start.6
  33.1 58.2 %all-to-all-start.1 = ((f32[128,64,128]{2,1,0:T(8,128)}), f32[128,64,128]{2,1,0:T(8,128)}, u32[]{:S(2)}, u32[]{:S(2)}) async-start(f32[128,64,128]{2,1,0:T(8,128)} %copy-done.6), calls=%async_computation.1 | async-start | bytes 8388608 | tf_op jit(solution)/shard_map/all_to_all | solution.py:314
  38.4 53.0 %copy-start.4 = (bf16[6,256,256]{2,1,0:T(8,128)(2,1)S(1)}, bf16[6,256,256]{2,1,0:T(8,128)(2,1)}, u32[]{:S(2)}) copy-start(bf16[6,256,256]{2,1,0:T(8,128)(2,1)} %constant.69.clone.tab) | copy-start | bytes 2359300
  91.4 2.2 copy-start
  93.6 66.8 %copy-start.7 = (f32[16,128,512]{2,1,0:T(8,128)S(1)}, f32[16,128,512]{2,1,0:T(8,128)}, u32[]{:S(2)}) copy-start(f32[16,128,512]{2,1,0:T(8,128)} %prev.1) | copy-start | bytes 12582916
  103.5 56.9 %copy-start.2 = (f32[16,128,512]{2,1,0:T(8,128)S(1)}, f32[16,128,512]{2,1,0:T(8,128)}, u32[]{:S(2)}) copy-start(f32[16,128,512]{2,1,0:T(8,128)} %p.5) | copy-start | bytes 12582916
  103.5 56.9 %copy-start.5 = (f32[16,128,512]{2,1,0:T(8,128)S(1)}, f32[16,128,512]{2,1,0:T(8,128)}, u32[]{:S(2)}) copy-start(f32[16,128,512]{2,1,0:T(8,128)} %speed.3) | copy-start | bytes 12582916
  165.6 56.9 %copy-start.1 = (f32[4,512,512]{2,1,0:T(8,128)S(1)}, f32[4,512,512]{2,1,0:T(8,128)}, u32[]{:S(2)}) copy-start(f32[4,512,512]{2,1,0:T(8,128)} %fusion.13.sym) | copy-start | bytes 12582916
  230.0 56.9 %copy-start.8 = (f32[16,128,512]{2,1,0:T(8,128)S(1)}, f32[16,128,512]{2,1,0:T(8,128)}, u32[]{:S(2)}) copy-start(f32[16,128,512]{2,1,0:T(8,128)} %get-tuple-element.7.cur) | copy-start | bytes 12582916
where the time goes:
time: 291 us
  blocking collectives  171 us (59%)
  waiting for transfers between devices  58.4 us (20%)
  Pallas kernels  31.3 us (11%)
  starting transfers between devices  16.7 us (6%)
  local copies, waits for them, and re-layouts  8.35 us (3%)
  other arithmetic  4.33 us (1%)
    all_to_all x3, blocking collectives, exchange(): lax.all_to_all(array, SLAB_PEN, split_axis=0, concat_axis=0, tiled=True)  171 us
    all_to_all x2, waiting for transfers between devices, exchange(): lax.all_to_all(array, SLAB_PEN, split_axis=0, concat_axis=0, tiled=True)  58.4 us
    pallas_call x2, Pallas kernels, spectral(): pl.pallas_call(spectral_kernel, grid=(2,), in_specs=[cube, planes2, TAB],...  17.4 us
    all_to_all x2, starting transfers between devices, exchange(): lax.all_to_all(array, SLAB_PEN, split_axis=0, concat_axis=0, tiled=True)  16.7 us
    unnamed x22, local copies, waits for them, and re-layouts  6.82 us
  transfers between devices with their start and end apart: 2, of which 2 were waited for; matrix products, arithmetic and copies ran while one was open for 1% of the time, Pallas kernels for 0%

commit v1 on v0

--- a/solution.py
+++ b/solution.py
@@ -162,13 +162,9 @@
         part = pl.ds(i * ZB, ZB)
         return pltpu.make_async_copy(p.at[part], p_v.at[part], sems.at[i])
 
-    @pl.when(step == 0)
-    def _():
-        for i in range(16 // ZB):
-            copy(i).start()
-        fill_maps(offs, vox, tcol, gathered, zmap, vmap0, vmap1)
-
-    copy(step).wait()
+    copy(0).start()
+    fill_maps(offs, vox, tcol, gathered, zmap, vmap0, vmap1)
+    copy(0).wait()
     base = step * ZB
     forward_x(
         [
@@ -187,11 +183,9 @@
 
 
 def wait_all(scratch, target, sems):
-    @pl.when(pl.program_id(0) == 16 // ZB - 1)
-    def _():
-        for group in range(16 // PZ):
-            part = pl.ds(group * PZ, PZ)
-            pltpu.make_async_copy(scratch.at[part], target.at[part], sems.at[group]).wait()
+    for group in range(16 // PZ):
+        part = pl.ds(group * PZ, PZ)
+        pltpu.make_async_copy(scratch.at[part], target.at[part], sems.at[group]).wait()
 
 
 def own_planes(i):

time: 291 us -> 291 us (level)
  no operation moved by 1% of the time
where the time goes in v1:
time: 291 us
  blocking collectives  171 us (59%)
  waiting for transfers between devices  58.4 us (20%)
  Pallas kernels  31.3 us (11%)
  starting transfers between devices  16.7 us (6%)
  local copies, waits for them, and re-layouts  8.35 us (3%)
  other arithmetic  4.33 us (1%)
    all_to_all x3, blocking collectives, exchange(): lax.all_to_all(array, SLAB_PEN, split_axis=0, concat_axis=0, tiled=True)  171 us
    all_to_all x2, waiting for transfers between devices, exchange(): lax.all_to_all(array, SLAB_PEN, split_axis=0, concat_axis=0, tiled=True)  58.4 us
    pallas_call x2, Pallas kernels, spectral(): pl.pallas_call(spectral_kernel, grid=(2,), in_specs=[cube, planes2, TAB],...  17.4 us
    all_to_all x2, starting transfers between devices, exchange(): lax.all_to_all(array, SLAB_PEN, split_axis=0, concat_axis=0, tiled=True)  16.7 us
    unnamed x22, local copies, waits for them, and re-layouts  6.82 us
  transfers between devices with their start and end apart: 2, of which 2 were waited for; matrix products, arithmetic and copies ran while one was open for 1% of the time, Pallas kernels for 0%

profile of v1, /device:TPU:1, one launch (start us, length us, event | category | flops | bytes accessed | tf_op | source)
XLA Modules:
  0.0 290.8 jit_solution(7600724428848716920)
XLA Ops:
  0.6 1.4 broadcast_in_dim.2
  2.0 11.5 %all-to-all-start = ((f32[128,2,16]{2,1,0:T(2,128)}), f32[128,2,16]{2,1,0:T(2,128)S(1)}, u32[]{:S(2)}, u32[]{:S(2)}) async-start(f32[128,2,16]{2,1,0:T(2,128)} %broadcast_in_dim.2), calls=%async_computation | async-start | bytes 262144 | tf_op jit(solution)/shard_map/all_to_all | solution.py:308
  13.5 0.1 pad_add_fusion.offs
  13.6 9.7 %all-to-all-done = f32[128,2,16]{2,1,0:T(2,128)S(1)} async-done(((f32[128,2,16]{2,1,0:T(2,128)}), f32[128,2,16]{2,1,0:T(2,128)S(1)}, u32[]{:S(2)}, u32[]{:S(2)}) %all-to-all-start) | async-done | bytes 16416 | tf_op jit(solution)/shard_map/all_to_all | solution.py:308
  23.3 0.1 copy.10
  23.4 0.1 copy.11.gathered
  23.5 0.0 copy-start.3
  23.5 1.1 copy-done.3
  24.6 0.0 copy-start.9
  24.6 0.8 copy-done.9
  25.4 0.0 copy-start.10
  25.4 0.7 copy-done.10
  26.1 5.0 %first.1 = (s32[128,512]{1,0:T(8,128)S(1)}, f32[128,512]{1,0:T(8,128)S(1)}, f32[128,512]{1,0:T(8,128)S(1)}, f32[128,64,128]{2,1,0:T(8,128)S(1)}) custom-call(s32[2]{0:T(128)S(1)} %pad_add_fusion.offs, s32[3,2048]{1,0:T(4,128)S(1)} %copy-done.9, s32[1,2048]{1,0:T(1,128)S(1)} %bitcast.11, f32[128,32]{1,0:T(8,128)S(1)} %copy.11.gathered, f32[16,128,512]{2,1,0:T(8,128)} %p.5, ...), custom_call_target="tpu_custom_call" | custom-call | tf_op jit(solution)/shard_map/first/pallas_call | solution.py:321
  31.1 0.0 copy-start.6
  31.1 2.0 copy-done.6
  33.1 5.2 %all-to-all-start.1 = ((f32[128,64,128]{2,1,0:T(8,128)}), f32[128,64,128]{2,1,0:T(8,128)}, u32[]{:S(2)}, u32[]{:S(2)}) async-start(f32[128,64,128]{2,1,0:T(8,128)} %copy-done.6), calls=%async_computation.1 | async-start | bytes 8388608 | tf_op jit(solution)/shard_map/all_to_all | solution.py:308
  38.4 0.0 copy-start.4
  38.5 0.1 broadcast_add_fusion
  38.6 4.1 %fusion.13.sym = f32[4,512,512]{2,1,0:T(8,128)} fusion(f32[4]{0:T(128)S(1)} %multiply_multiply_fusion.1, f32[512,512]{1,0:T(8,128)S(1)} %broadcast_add_fusion), kind=kLoop, calls=%fused_computation.16 | loop fusion | flops 19922944 | bytes 5242896 | tf_op jit(solution)/shard_map/mul | solution.py:300
  42.7 48.7 %all-to-all-done.1 = f32[128,64,128]{2,1,0:T(8,128)} async-done(((f32[128,64,128]{2,1,0:T(8,128)}), f32[128,64,128]{2,1,0:T(8,128)}, u32[]{:S(2)}, u32[]{:S(2)}) %all-to-all-start.1) | async-done | bytes 4194336 | tf_op jit(solution)/shard_map/all_to_all | solution.py:308
  91.4 0.0 copy-done.4
  91.4 0.0 copy-start
  91.4 2.2 copy-done
  93.6 0.0 copy-start.7
  93.6 9.9 %spectral.2 = f32[32,4,64,128]{3,2,1,0:T(8,128)S(1)} custom-call(f32[32,4,64,128]{3,2,1,0:T(8,128)} %bitcast.4.arr, f32[4,512,512]{2,1,0:T(8,128)S(1)} %copy-done, bf16[6,256,256]{2,1,0:T(8,128)(2,1)S(1)} %copy-done.4), custom_call_target="tpu_custom_call" | custom-call | tf_op jit(solution)/shard_map/spectral/pallas_call | solution.py:342
  103.5 0.0 copy-start.2
  103.5 0.0 copy-start.5
  103.5 56.9 %all_to_all.25.arr = f32[128,64,128]{2,1,0:T(8,128)S(1)} all-to-all(f32[128,64,128]{2,1,0:T(8,128)S(1)} %bitcast.10), channel_id=1, replica_groups=mesh['slab_0'=4,'slab_1'=4,'slab_2'=2,'pen'=4] {'slab_0','slab_1','slab_..., dimensions={0} | all-to-all | bytes 8388608 | tf_op jit(solution)/shard_map/all_to_all | solution.py:308
  160.4 0.0 copy-done.7
  160.4 0.0 copy-done.2
  160.4 0.0 copy-done.5
  160.4 5.1 %middle.1 = (f32[16,128,512]{2,1,0:T(8,128)}, f32[128,64,128]{2,1,0:T(8,128)S(1)}) custom-call(f32[128,64,128]{2,1,0:T(8,128)S(1)} %all_to_all.25.arr, f32[16,128,512]{2,1,0:T(8,128)S(1)} %copy-done.7, f32[16,128,512]{2,1,0:T(8,128)S(1)} %copy-done.5, f32[16,128,512]{2,1,0:T(8,128)S(1)} %copy-done.2, s32[128,512]{1,0:T(8,128)S(1)} %get-tuple-element.9.zmap, ...), custom_call_target="tpu_custom_call" | custom-call | tf_op jit(solution)/shard_map/middle/pallas_call | solution.py:353
  165.6 0.0 copy-start.1
  165.6 56.9 %all_to_all.26 = f32[128,64,128]{2,1,0:T(8,128)S(1)} all-to-all(f32[128,64,128]{2,1,0:T(8,128)S(1)} %get-tuple-element.12), channel_id=1, replica_groups=mesh['slab_0'=4,'slab_1'=4,'slab_2'=2,'pen'=4] {'slab_0','slab_1','slab_..., dimensions={0} | all-to-all | bytes 8388608 | tf_op jit(solution)/shard_map/all_to_all | solution.py:308
  222.5 0.0 copy-done.1
  222.5 7.5 %spectral.3 = f32[32,4,64,128]{3,2,1,0:T(8,128)S(1)} custom-call(f32[32,4,64,128]{3,2,1,0:T(8,128)S(1)} %bitcast.8, f32[4,512,512]{2,1,0:T(8,128)S(1)} %copy-done.1, bf16[6,256,256]{2,1,0:T(8,128)(2,1)S(1)} %copy-done.4), custom_call_target="tpu_custom_call" | custom-call | tf_op jit(solution)/shard_map/spectral/pallas_call | solution.py:342
  230.0 0.0 copy-start.8
  230.0 56.9 %all_to_all.27.arr = f32[128,64,128]{2,1,0:T(8,128)S(1)} all-to-all(f32[128,64,128]{2,1,0:T(8,128)S(1)} %bitcast.9), channel_id=1, replica_groups=mesh['slab_0'=4,'slab_1'=4,'slab_2'=2,'pen'=4] {'slab_0','slab_1','slab_..., dimensions={0} | all-to-all | bytes 8388608 | tf_op jit(solution)/shard_map/all_to_all | solution.py:308
  287.0 0.0 copy-done.8
  287.0 3.7 %last.1 = f32[16,128,512]{2,1,0:T(8,128)} custom-call(f32[128,64,128]{2,1,0:T(8,128)S(1)} %all_to_all.27.arr, f32[16,128,512]{2,1,0:T(8,128)S(1)} %copy-done.8, f32[16,128,512]{2,1,0:T(8,128)S(1)} %copy-done.5, f32[16,128,512]{2,1,0:T(8,128)S(1)} %copy-done.2, s32[128,512]{1,0:T(8,128)S(1)} %get-tuple-element.9.zmap, ...), custom_call_target="tpu_custom_call" | custom-call | tf_op jit(solution)/shard_map/last/pallas_call | solution.py:364
  (2 shorter events, 0.0 us)
Async XLA Ops:
  2.0 21.3 %all-to-all-start = ((f32[128,2,16]{2,1,0:T(2,128)}), f32[128,2,16]{2,1,0:T(2,128)S(1)}, u32[]{:S(2)}, u32[]{:S(2)}) async-start(f32[128,2,16]{2,1,0:T(2,128)} %broadcast_in_dim.2), calls=%async_computation | async-start | bytes 262144 | tf_op jit(solution)/shard_map/all_to_all | solution.py:308
  23.5 1.1 copy-start.3
  24.6 0.8 copy-start.9
  25.4 0.7 copy-start.10
  31.1 2.0 copy-start.6
  33.1 58.2 %all-to-all-start.1 = ((f32[128,64,128]{2,1,0:T(8,128)}), f32[128,64,128]{2,1,0:T(8,128)}, u32[]{:S(2)}, u32[]{:S(2)}) async-start(f32[128,64,128]{2,1,0:T(8,128)} %copy-done.6), calls=%async_computation.1 | async-start | bytes 8388608 | tf_op jit(solution)/shard_map/all_to_all | solution.py:308
  38.4 53.0 %copy-start.4 = (bf16[6,256,256]{2,1,0:T(8,128)(2,1)S(1)}, bf16[6,256,256]{2,1,0:T(8,128)(2,1)}, u32[]{:S(2)}) copy-start(bf16[6,256,256]{2,1,0:T(8,128)(2,1)} %constant.69.clone.tab) | copy-start | bytes 2359300
  91.4 2.2 copy-start
  93.6 66.8 %copy-start.7 = (f32[16,128,512]{2,1,0:T(8,128)S(1)}, f32[16,128,512]{2,1,0:T(8,128)}, u32[]{:S(2)}) copy-start(f32[16,128,512]{2,1,0:T(8,128)} %prev.1) | copy-start | bytes 12582916
  103.5 56.9 %copy-start.2 = (f32[16,128,512]{2,1,0:T(8,128)S(1)}, f32[16,128,512]{2,1,0:T(8,128)}, u32[]{:S(2)}) copy-start(f32[16,128,512]{2,1,0:T(8,128)} %p.5) | copy-start | bytes 12582916
  103.5 56.9 %copy-start.5 = (f32[16,128,512]{2,1,0:T(8,128)S(1)}, f32[16,128,512]{2,1,0:T(8,128)}, u32[]{:S(2)}) copy-start(f32[16,128,512]{2,1,0:T(8,128)} %speed.3) | copy-start | bytes 12582916
  165.6 56.9 %copy-start.1 = (f32[4,512,512]{2,1,0:T(8,128)S(1)}, f32[4,512,512]{2,1,0:T(8,128)}, u32[]{:S(2)}) copy-start(f32[4,512,512]{2,1,0:T(8,128)} %fusion.13.sym) | copy-start | bytes 12582916
  230.0 56.9 %copy-start.8 = (f32[16,128,512]{2,1,0:T(8,128)S(1)}, f32[16,128,512]{2,1,0:T(8,128)}, u32[]{:S(2)}) copy-start(f32[16,128,512]{2,1,0:T(8,128)} %get-tuple-element.7.cur) | copy-start | bytes 12582916
